TPU v7x, 256 devices: a whole 4x4x8 slice. The times are simulated.
256 devices in a mesh: seq: 32 (over x, z_lo, core), head: 8 (over y, z_hi).
Axes of the slice: x: 4, y: 4, z: 8 (z_hi: 2, z_lo: 4; z = z_hi * 4 + z_lo), core: 2. Of those that a mesh axis runs over, the one named last changes fastest.
Arguments:
- tokens: bfloat16 [16384, 1024], P('seq'), may hold values from -6 to 6
- mem_query_w: bfloat16 [1024, 1024], P(None, 'head'), may hold values from -0.1875 to 0.1875
- mem_key_w: bfloat16 [1024, 1024], P(None, 'head'), may hold values from -0.1875 to 0.1875
- mem_value_w: bfloat16 [1024, 1024], P(None, 'head'), may hold values from -0.1875 to 0.1875
- mem_in: float32 [1024, 1024], P(None, 'head'), may hold values from -0.1875 to 0.1875
- mem_out: float32 [1024, 1024], P('head'), may hold values from -0.1875 to 0.1875
- forget_levels: float32 [16, 1024], P(None, 'head'), may hold values from 0.003 to 0.3
- momentum_levels: float32 [16, 1024], P(None, 'head'), may hold values from 0.2 to 0.9
- step_levels: float32 [16, 1024], P(None, 'head'), may hold values from 0.02 to 0.2
- plan: int32 [32], P('seq'), may hold values from 0 to 15
- norm_gain: float32 [1024], replicated, may hold values from 0.5 to 1.5
- attn_query_w: bfloat16 [1024, 1024], P(None, 'head'), may hold values from -1 to 1
- attn_key_w: bfloat16 [1024, 1024], P(None, 'head'), may hold values from -4 to 4
- attn_value_w: bfloat16 [1024, 1024], P(None, 'head'), may hold values from -0.1875 to 0.1875
- attn_out_w: bfloat16 [1024, 1024], P('head'), may hold values from -0.25 to 0.25
Outputs:
- layer_out: bfloat16 [16384, 1024], P('seq', 'head')
All inputs are finite; a program needn't handle non-finite values.
Results may differ from a plain program's by a relative error of at most 0.014.
Values may be sent and summed in bfloat16 or wider, within the bound.
A program may use at most 128 MiB of HBM per device.

v0:
```python
import jax
import jax.numpy as jnp
from jax import lax
from jax.sharding import Mesh
from jax.sharding import PartitionSpec as P

HEAD_DIM = 64
SPAN = 8
SEQ = ("seq_0", "seq_1", "seq_2")
epsilon = 1e-06


def split_up(value, dim, length):
    before, after = (value.shape[:dim], value.shape[dim + 1 :])
    return jnp.moveaxis(value.reshape(*before, length, -1, *after), dim, 0)


def sent_and_summed(value, axis, dim):
    length = lax.axis_size(axis)
    blocks = lax.all_to_all(split_up(value, dim, length), axis, 0, 0, tiled=True)
    return jnp.sum(blocks, axis=0)


def filled_with(value, identity):
    return jax.tree.map(
        lambda a, e: jnp.broadcast_to(jnp.asarray(e, a.dtype), a.shape), value, identity
    )


def gathered_once(value, axis):
    leaves = jax.tree.leaves(value)
    sequence = sorted(range(len(leaves)), key=lambda k: -leaves[k].size)
    width = (1, *leaves[sequence[0]].shape)[-1]
    lines = [
        jnp.pad(leaves[k].reshape(-1), (0, -leaves[k].size % width)).reshape(-1, width)
        for k in sequence
    ]
    both, at, found = (lax.all_gather(jnp.concatenate(lines), axis), 0, {})
    for k, line in zip(sequence, lines):
        section = both[:, at : at + len(line)].reshape(len(both), -1)
        found[k] = section[:, : leaves[k].size].reshape(-1, *leaves[k].shape)
        at += len(line)
    numbers = iter(range(len(leaves)))
    return jax.tree.map(lambda _: found[next(numbers)], value)


def carried_in(value, axes, combine, identity):
    before = start = filled_with(value, identity)
    running = value
    for axis in reversed(axes):
        length, index = (lax.axis_size(axis), lax.axis_index(axis))
        pieces = gathered_once(running, axis)
        inside, running = (start, start)
        for k in range(length):
            passed = k < index
            running = combine(running, jax.tree.map(lambda part: part[k], pieces))
            inside = jax.tree.map(lambda new, old: jnp.where(passed, new, old), running, inside)
        before = combine(inside, before)
    return before


def shifted(value, axis, by):
    length = lax.axis_size(axis)
    pairs = [(i, i + by) for i in range(length) if 0 <= i + by < length]
    return lax.ppermute(value, axis, pairs)


def sum_at_owner(value, axis, dim):
    length = lax.axis_size(axis)
    blocks = lax.all_to_all(split_up(value, dim, length), axis, 0, 0, tiled=True)
    return jnp.sum(blocks.astype(jnp.float32), axis=0)


def silu_slope(values):
    sigmoid = jax.nn.sigmoid(values)
    return sigmoid * (1.0 + values * (1.0 - sigmoid))


def project(left, weight):
    return jnp.dot(left, weight, preferred_element_type=jnp.float32).astype(jnp.bfloat16)


def normalize(retrieved, norm_gain):
    mean_square = jnp.mean(retrieved * retrieved, axis=-1, keepdims=True)
    return (retrieved * lax.rsqrt(mean_square + epsilon) * norm_gain).astype(jnp.bfloat16)


def lookup(table, chosen):
    matches = jnp.arange(table.shape[0], dtype=jnp.int32)[:, None] == chosen
    return jnp.sum(jnp.where(matches, table, 0.0), axis=0)


def as_columns(vector):
    return vector[..., None, :]


def as_rows(vector):
    return vector[..., :, None]


def compose(earlier, later):
    (
        prior_decay,
        prior_cross,
        prior_keep,
        prior_speed_in,
        prior_speed_out,
        prior_weight_in,
        prior_weight_out,
    ) = earlier
    (
        after_decay,
        after_cross,
        after_keep,
        after_speed_in,
        after_speed_out,
        after_weight_in,
        after_weight_out,
    ) = later
    decay = after_decay * prior_decay
    cross = after_cross * prior_decay + after_keep * prior_cross
    keep = after_keep * prior_keep
    speed_in = as_columns(after_decay) * prior_speed_in + after_speed_in
    speed_out = as_rows(after_decay) * prior_speed_out + after_speed_out
    weight_in = (
        as_columns(after_cross) * prior_speed_in
        + as_columns(after_keep) * prior_weight_in
        + after_weight_in
    )
    weight_out = (
        as_rows(after_cross) * prior_speed_out
        + as_rows(after_keep) * prior_weight_out
        + after_weight_out
    )
    return (decay, cross, keep, speed_in, speed_out, weight_in, weight_out)


def window_attend(query, keys, values, block_index):
    query_count = query.shape[0]
    key_count = keys.shape[0]
    span_rows = key_count - query_count
    distance = (
        span_rows
        + jnp.arange(query_count, dtype=jnp.int32)[:, None]
        - jnp.arange(key_count, dtype=jnp.int32)[None, :]
    )
    key_pos = (block_index * query_count - span_rows + jnp.arange(key_count, dtype=jnp.int32))[
        None, :
    ]
    allowed = (distance >= 0) & (distance < span_rows) & (key_pos >= 0)
    contexts = []
    for head_number in range(query.shape[1] // HEAD_DIM):
        low_col = head_number * HEAD_DIM
        scores = jnp.einsum(
            "qd,kd->qk",
            query[:, low_col : low_col + HEAD_DIM],
            keys[:, low_col : low_col + HEAD_DIM],
            preferred_element_type=jnp.float32,
        ) * HEAD_DIM ** (-0.5)
        scores = jnp.where(allowed, scores, -1e30)
        row_peak = jnp.max(scores, axis=-1, keepdims=True)
        weights = jnp.exp(scores - row_peak)
        probabilities = (weights / jnp.sum(weights, axis=-1, keepdims=True)).astype(jnp.bfloat16)
        contexts.append(
            jnp.dot(
                probabilities,
                values[:, low_col : low_col + HEAD_DIM],
                preferred_element_type=jnp.float32,
            ).astype(jnp.bfloat16)
        )
    return jnp.concatenate(contexts, axis=1)


def shards(
    tokens,
    mem_query_w,
    mem_key_w,
    mem_value_w,
    mem_in,
    mem_out,
    forget_levels,
    momentum_levels,
    step_levels,
    plan,
    norm_gain,
    attn_query_w,
    attn_key_w,
    attn_value_w,
    attn_out_w,
):
    tok_rows = tokens.shape[0]
    share_rows = tok_rows // lax.axis_size("head")
    my_start = lax.axis_index("head") * share_rows
    mem_query, mem_key, mem_value = (
        lax.all_gather(project(tokens, mem_query_w), "head", axis=1, tiled=True),
        lax.all_gather(project(tokens, mem_key_w), "head", axis=1, tiled=True),
        lax.all_gather(project(tokens, mem_value_w), "head", axis=1, tiled=True),
    )
    keys_wide = mem_key.astype(jnp.float32)
    pre_act = jnp.dot(keys_wide, mem_in)
    hidden = jax.nn.silu(pre_act)
    predicted = sent_and_summed(jnp.dot(hidden, mem_out), "head", 0)
    value_share = lax.dynamic_slice_in_dim(mem_value, my_start, share_rows, 0).astype(jnp.float32)
    residual_err = lax.all_gather(
        2.0 / tok_rows * (predicted - value_share), "head", axis=0, tiled=True
    )
    grad_out = jnp.dot(hidden.T, residual_err)
    slope_term = jnp.dot(residual_err, mem_out.T) * silu_slope(pre_act)
    grad_in = jnp.dot(keys_wide.T, slope_term)
    chosen = plan[0]
    forget = lookup(forget_levels, chosen)
    momentum = lookup(momentum_levels, chosen)
    step_rate = lookup(step_levels, chosen)
    change_in = -as_columns(step_rate) * grad_in
    change_out = -as_rows(step_rate) * grad_out
    element = (momentum, momentum, 1.0 - forget, change_in, change_out, change_in, change_out)
    identity = (
        jnp.ones_like(momentum),
        jnp.zeros_like(momentum),
        jnp.ones_like(momentum),
        jnp.zeros_like(grad_in),
        jnp.zeros_like(grad_out),
        jnp.zeros_like(grad_in),
        jnp.zeros_like(grad_out),
    )
    entering = carried_in(element, SEQ, compose, identity)
    weight_in = as_columns(entering[2]) * mem_in + entering[5]
    weight_out = as_rows(entering[2]) * mem_out + entering[6]
    query_hidden = jax.nn.silu(jnp.dot(mem_query.astype(jnp.float32), weight_in))
    retrieved = sent_and_summed(jnp.dot(query_hidden, weight_out), "head", 0)
    normed = lax.all_gather(normalize(retrieved, norm_gain), "head", axis=0, tiled=True)
    att_query = project(normed, attn_query_w)
    att_key = project(normed, attn_key_w)
    att_value = project(normed, attn_value_w)
    earlier = []
    for distance in range(SPAN, 0, -1):
        earlier.append(shifted((att_key, att_value), SEQ, distance))
    key_window = jnp.concatenate([received[0] for received in earlier] + [att_key], axis=0)
    value_window = jnp.concatenate([received[1] for received in earlier] + [att_value], axis=0)
    context = window_attend(att_query, key_window, value_window, lax.axis_index(SEQ))
    partial_out = jnp.dot(context, attn_out_w, preferred_element_type=jnp.float32)
    return sum_at_owner(partial_out.astype(jnp.bfloat16), "head", 1).astype(jnp.bfloat16)


def solution(mesh):
    split = Mesh(
        mesh.devices.reshape(4, 4, 2, mesh.shape["head"]), ("seq_0", "seq_1", "seq_2", "head")
    )
    in_specs = (
        P(SEQ, None),
        P(None, "head"),
        P(None, "head"),
        P(None, "head"),
        P(None, "head"),
        P("head", None),
        P(None, "head"),
        P(None, "head"),
        P(None, "head"),
        P(SEQ),
        P(),
        P(None, "head"),
        P(None, "head"),
        P(None, "head"),
        P("head", None),
    )
    out_specs = P(SEQ, "head")
    return jax.shard_map(
        shards, mesh=split, in_specs=in_specs, out_specs=out_specs, check_vma=False
    )
```

profile of v0, /device:TPU:33, one launch (start us, length us, event | category | flops | bytes accessed | tf_op | source)
XLA Modules:
  0.0 816.8 jit_solution(12139986413345933075)
XLA Ops:
  9.8 61.9 %all-gather.17.cloned.1.call-done = bf16[512,1024]{1,0:T(8,128)(2,1)} async-done(((bf16[512,128]{1,0:T(8,128)(2,1)}), bf16[512,1024]{1,0:T(8,128)(2,1)}) %all-gather.17.cloned.1.call-update) | async-done | bytes 1048592 | tf_op jit(solution)/shard_map/all_gather | solution.py:196
  76.0 3.7 all-to-all-start
  81.0 54.1 %all-to-all-done = f32[8,64,1024]{2,1,0:T(8,128)S(1)} async-done(((f32[8,64,1024]{2,1,0:T(8,128)}), f32[8,64,1024]{2,1,0:T(8,128)S(1)}, u32[]{:S(2)}, u32[]{:S(2)}) %all-to-all-start) | async-done | bytes 2097184 | tf_op jit(solution)/shard_map/all_to_all | solution.py:20
  135.3 23.0 %all-gather.19.cloned.1.call-done = bf16[512,1024]{1,0:T(8,128)(2,1)} async-done(((bf16[512,128]{1,0:T(8,128)(2,1)}), bf16[512,1024]{1,0:T(8,128)(2,1)}) %all-gather.19.cloned.1.call-update) | async-done | bytes 1048592 | tf_op jit(solution)/shard_map/all_gather | solution.py:197
  160.7 57.5 %all-gather.21.cloned.1.call-done = bf16[512,1024]{1,0:T(8,128)(2,1)} async-done(((bf16[64,1024]{1,0:T(8,128)(2,1)}), bf16[512,1024]{1,0:T(8,128)(2,1)}) %all-gather.21.cloned.1.call-update) | async-done | bytes 1048592 | tf_op jit(solution)/shard_map/all_gather | solution.py:204
  222.7 4.1 concatenate.18
  226.8 17.6 %all-gather.25.cloned.1.call-done = f32[2,4099,128]{2,1,0:T(8,128)} async-done(((f32[1,4099,128]{2,1,0:T(8,128)}), f32[2,4099,128]{2,1,0:T(8,128)}) %all-gather.25.cloned.1.call-update) | async-done | bytes 4197392 | tf_op jit(solution)/shard_map/all_gather | solution.py:38
  251.5 4.1 concatenate.19
  255.6 154.2 %all-gather.27.cloned.1.call-done = f32[4,4099,128]{2,1,0:T(8,128)} async-done(((f32[1,4099,128]{2,1,0:T(8,128)}), f32[4,4099,128]{2,1,0:T(8,128)}) %all-gather.27.cloned.1.call-update) | async-done | bytes 8394768 | tf_op jit(solution)/shard_map/all_gather | solution.py:38
  418.9 4.0 bitcast_add_fusion
  423.0 4.1 concatenate.20
  446.6 65.9 %all-gather.29.cloned.1.call-done = f32[4,4099,128]{2,1,0:T(8,128)} async-done(((f32[1,4099,128]{2,1,0:T(8,128)}), f32[4,4099,128]{2,1,0:T(8,128)}) %all-gather.29.cloned.1.call-update) | async-done | bytes 8394768 | tf_op jit(solution)/shard_map/all_gather | solution.py:38
  526.8 48.5 %all-gather.15.cloned.1.call-done = bf16[512,1024]{1,0:T(8,128)(2,1)} async-done(((bf16[512,128]{1,0:T(8,128)(2,1)}), bf16[512,1024]{1,0:T(8,128)(2,1)}) %all-gather.15.cloned.1.call-update) | async-done | bytes 1048592 | tf_op jit(solution)/shard_map/all_gather | solution.py:195
  575.3 11.3 %fusion.57 = f32[512,1024]{1,0:T(8,128)} fusion(f32[128,1024]{1,0:T(8,128)} %squeeze.275, f32[128,1024]{1,0:T(8,128)} %squeeze.274, f32[128,1024]{1,0:T(8,128)} %squeeze.273, f32[128,1024]{1,0:T(8,128)} %squeeze.272, f32[128,1024]{1,0:T(8,128)} %squeeze.271, f32[128,1024]{1,0:T(8,128)} %squeeze.270, f32[128,1024]{1,0:T(8,128)} %squeeze.269, ...), kind=kOutput, calls=%fused_computation.101 | convolution fusion | flops 287834112 | bytes 25205248 | tf_op jit(solution)/shard_map/dot_general | solution.py:230
  586.6 56.2 %all_to_all.15 = f32[8,64,1024]{2,1,0:T(8,128)S(1)} all-to-all(f32[8,64,1024]{2,1,0:T(8,128)} %bitcast.561), channel_id=1, replica_groups=mesh['seq_0'=4,'seq_1'=4,'seq_2'=2,'head'=8] {'head'}, dimensions={0} | all-to-all | bytes 4194304 | tf_op jit(solution)/shard_map/all_to_all | solution.py:20
  644.3 54.3 %all-gather.23.cloned.1.call-done = bf16[512,1024]{1,0:T(8,128)(2,1)} async-done(((bf16[64,1024]{1,0:T(8,128)(2,1)}), bf16[512,1024]{1,0:T(8,128)(2,1)}) %all-gather.23.cloned.1.call-update) | async-done | bytes 1048592 | tf_op jit(solution)/shard_map/all_gather | solution.py:231
  703.5 5.4 collective-permute-start.1
  708.9 3.6 collective-permute-start.2
  713.8 4.1 collective-permute-start.4
  731.5 8.3 %collective-permute-start.10 = (bf16[512,128]{1,0:T(8,128)(2,1)S(1)}, bf16[512,128]{1,0:T(8,128)(2,1)S(1)}, u32[]{:S(2)}, u32[]{:S(2)}) collective-permute-start(bf16[512,128]{1,0:T(8,128)(2,1)S(1)} %convolution_convert_fusion.1), channel_id=1, source_target_pairs={{0,48},{8,56},{16,64},{24,72},{32,80},{40,88},{48,96},{56,104},{64... | collective-permute-start | bytes 393224 | tf_op jit(solution)/shard_map/ppermute | solution.py:65
  744.2 4.3 fusion.356
  748.5 4.2 fusion.355
  752.7 4.3 collective-permute-start.13
  773.0 36.1 %all_to_all.16 = bf16[8,512,128]{2,1,0:T(8,128)(2,1)S(1)} all-to-all(bf16[8,512,128]{2,1,0:T(8,128)(2,1)S(1)} %bitcast.560), channel_id=1, replica_groups=mesh['seq_0'=4,'seq_1'=4,'seq_2'=2,'head'=8] {'head'}, dimensions={0} | all-to-all | bytes 2097152 | tf_op jit(solution)/shard_map/all_to_all | solution.py:70
  (210 shorter events, 106.8 us)
Async XLA Ops:
  6.5 65.2 %all-gather.17.cloned.1.call-start = ((), (), s32[]{:S(2)}) async-start(), calls=%async_computation.4 | async-start | bytes 1179648 | tf_op jit(solution)/shard_map/all_gather | solution.py:196
  76.0 59.1 %all-to-all-start = ((f32[8,64,1024]{2,1,0:T(8,128)}), f32[8,64,1024]{2,1,0:T(8,128)S(1)}, u32[]{:S(2)}, u32[]{:S(2)}) async-start(f32[8,64,1024]{2,1,0:T(8,128)} %bitcast.559), calls=%async_computation | async-start | bytes 4194304 | tf_op jit(solution)/shard_map/all_to_all | solution.py:20
  79.8 78.5 %all-gather.19.cloned.1.call-start = ((), (), s32[]{:S(2)}) async-start(), calls=%async_computation.5 | async-start | bytes 1179648 | tf_op jit(solution)/shard_map/all_gather | solution.py:197
  80.9 137.3 %all-gather.21.cloned.1.call-start = ((), (), s32[]{:S(2)}) async-start(), calls=%async_computation.6 | async-start | bytes 1179648 | tf_op jit(solution)/shard_map/all_gather | solution.py:204
  159.8 84.5 %all-gather.25.cloned.1.call-start = ((), (), s32[]{:S(2)}) async-start(), calls=%async_computation.8 | async-start | bytes 6303744 | tf_op jit(solution)/shard_map/all_gather | solution.py:38
  226.8 183.1 %all-gather.27.cloned.1.call-start = ((), (), s32[]{:S(2)}) async-start(), calls=%async_computation.9 | async-start | bytes 10506240 | tf_op jit(solution)/shard_map/all_gather | solution.py:38
  255.6 256.9 %all-gather.29.cloned.1.call-start = ((), (), s32[]{:S(2)}) async-start(), calls=%async_computation.10 | async-start | bytes 10506240 | tf_op jit(solution)/shard_map/all_gather | solution.py:38
  427.1 148.2 %all-gather.15.cloned.1.call-start = ((), (), s32[]{:S(2)}) async-start(), calls=%async_computation.3 | async-start | bytes 1179648 | tf_op jit(solution)/shard_map/all_gather | solution.py:195
  428.3 270.3 %all-gather.23.cloned.1.call-start = ((), (), s32[]{:S(2)}) async-start(), calls=%async_computation.7 | async-start | bytes 1179648 | tf_op jit(solution)/shard_map/all_gather | solution.py:231
  700.3 19.7 %collective-permute-start = (bf16[512,128]{1,0:T(8,128)(2,1)S(1)}, bf16[512,128]{1,0:T(8,128)(2,1)S(1)}, u32[]{:S(2)}, u32[]{:S(2)}) collective-permute-start(bf16[512,128]{1,0:T(8,128)(2,1)S(1)} %convolution_convert_fusion.2), channel_id=1, source_target_pairs={{0,64},{8,72},{16,80},{24,88},{32,96},{40,104},{48,112},{56,120},{... | collective-permute-start | bytes 393224 | tf_op jit(solution)/shard_map/ppermute | solution.py:65
  703.5 19.7 %collective-permute-start.1 = (bf16[512,128]{1,0:T(8,128)(2,1)S(1)}, bf16[512,128]{1,0:T(8,128)(2,1)S(1)}, u32[]{:S(2)}, u32[]{:S(2)}) collective-permute-start(bf16[512,128]{1,0:T(8,128)(2,1)S(1)} %convolution_convert_fusion.2), channel_id=1, source_target_pairs={{0,56},{8,64},{16,72},{24,80},{32,88},{40,96},{48,104},{56,112},{6... | collective-permute-start | bytes 393224 | tf_op jit(solution)/shard_map/ppermute | solution.py:65
  708.9 16.6 %collective-permute-start.2 = (bf16[512,128]{1,0:T(8,128)(2,1)S(1)}, bf16[512,128]{1,0:T(8,128)(2,1)S(1)}, u32[]{:S(2)}, u32[]{:S(2)}) collective-permute-start(bf16[512,128]{1,0:T(8,128)(2,1)S(1)} %convolution_convert_fusion.2), channel_id=1, source_target_pairs={{0,48},{8,56},{16,64},{24,72},{32,80},{40,88},{48,96},{56,104},{64... | collective-permute-start | bytes 393224 | tf_op jit(solution)/shard_map/ppermute | solution.py:65
  712.5 16.3 %collective-permute-start.3 = (bf16[512,128]{1,0:T(8,128)(2,1)S(1)}, bf16[512,128]{1,0:T(8,128)(2,1)S(1)}, u32[]{:S(2)}, u32[]{:S(2)}) collective-permute-start(bf16[512,128]{1,0:T(8,128)(2,1)S(1)} %convolution_convert_fusion.2), channel_id=1, source_target_pairs={{0,40},{8,48},{16,56},{24,64},{32,72},{40,80},{48,88},{56,96},{64,... | collective-permute-start | bytes 393224 | tf_op jit(solution)/shard_map/ppermute | solution.py:65
  713.8 16.3 %collective-permute-start.4 = (bf16[512,128]{1,0:T(8,128)(2,1)S(1)}, bf16[512,128]{1,0:T(8,128)(2,1)S(1)}, u32[]{:S(2)}, u32[]{:S(2)}) collective-permute-start(bf16[512,128]{1,0:T(8,128)(2,1)S(1)} %convolution_convert_fusion.2), channel_id=1, source_target_pairs={{0,32},{8,40},{16,48},{24,56},{32,64},{40,72},{48,80},{56,88},{64,... | collective-permute-start | bytes 393224 | tf_op jit(solution)/shard_map/ppermute | solution.py:65
  720.1 11.4 %collective-permute-start.5 = (bf16[512,128]{1,0:T(8,128)(2,1)S(1)}, bf16[512,128]{1,0:T(8,128)(2,1)S(1)}, u32[]{:S(2)}, u32[]{:S(2)}) collective-permute-start(bf16[512,128]{1,0:T(8,128)(2,1)S(1)} %convolution_convert_fusion.2), channel_id=1, source_target_pairs={{0,24},{8,32},{16,40},{24,48},{32,56},{40,64},{48,72},{56,80},{64,... | collective-permute-start | bytes 393224 | tf_op jit(solution)/shard_map/ppermute | solution.py:65
  723.1 16.6 %collective-permute-start.6 = (bf16[512,128]{1,0:T(8,128)(2,1)S(1)}, bf16[512,128]{1,0:T(8,128)(2,1)S(1)}, u32[]{:S(2)}, u32[]{:S(2)}) collective-permute-start(bf16[512,128]{1,0:T(8,128)(2,1)S(1)} %convolution_convert_fusion.2), channel_id=1, source_target_pairs={{0,16},{8,24},{16,32},{24,40},{32,48},{40,56},{48,64},{56,72},{64,... | collective-permute-start | bytes 393224 | tf_op jit(solution)/shard_map/ppermute | solution.py:65
  725.4 17.1 %collective-permute-start.7 = (bf16[512,128]{1,0:T(8,128)(2,1)S(1)}, bf16[512,128]{1,0:T(8,128)(2,1)S(1)}, u32[]{:S(2)}, u32[]{:S(2)}) collective-permute-start(bf16[512,128]{1,0:T(8,128)(2,1)S(1)} %convolution_convert_fusion.2), channel_id=1, source_target_pairs={{0,8},{8,16},{16,24},{24,32},{32,40},{40,48},{48,56},{56,64},{64,7... | collective-permute-start | bytes 393224 | tf_op jit(solution)/shard_map/ppermute | solution.py:65
  728.8 23.9 %collective-permute-start.8 = (bf16[512,128]{1,0:T(8,128)(2,1)S(1)}, bf16[512,128]{1,0:T(8,128)(2,1)S(1)}, u32[]{:S(2)}, u32[]{:S(2)}) collective-permute-start(bf16[512,128]{1,0:T(8,128)(2,1)S(1)} %convolution_convert_fusion.1), channel_id=1, source_target_pairs={{0,64},{8,72},{16,80},{24,88},{32,96},{40,104},{48,112},{56,120},{... | collective-permute-start | bytes 393224 | tf_op jit(solution)/shard_map/ppermute | solution.py:65
  730.1 26.9 %collective-permute-start.9 = (bf16[512,128]{1,0:T(8,128)(2,1)S(1)}, bf16[512,128]{1,0:T(8,128)(2,1)S(1)}, u32[]{:S(2)}, u32[]{:S(2)}) collective-permute-start(bf16[512,128]{1,0:T(8,128)(2,1)S(1)} %convolution_convert_fusion.1), channel_id=1, source_target_pairs={{0,56},{8,64},{16,72},{24,80},{32,88},{40,96},{48,104},{56,112},{6... | collective-permute-start | bytes 393224 | tf_op jit(solution)/shard_map/ppermute | solution.py:65
  731.5 27.6 %collective-permute-start.10 = (bf16[512,128]{1,0:T(8,128)(2,1)S(1)}, bf16[512,128]{1,0:T(8,128)(2,1)S(1)}, u32[]{:S(2)}, u32[]{:S(2)}) collective-permute-start(bf16[512,128]{1,0:T(8,128)(2,1)S(1)} %convolution_convert_fusion.1), channel_id=1, source_target_pairs={{0,48},{8,56},{16,64},{24,72},{32,80},{40,88},{48,96},{56,104},{64... | collective-permute-start | bytes 393224 | tf_op jit(solution)/shard_map/ppermute | solution.py:65
  739.8 22.3 %collective-permute-start.11 = (bf16[512,128]{1,0:T(8,128)(2,1)S(1)}, bf16[512,128]{1,0:T(8,128)(2,1)S(1)}, u32[]{:S(2)}, u32[]{:S(2)}) collective-permute-start(bf16[512,128]{1,0:T(8,128)(2,1)S(1)} %convolution_convert_fusion.1), channel_id=1, source_target_pairs={{0,40},{8,48},{16,56},{24,64},{32,72},{40,80},{48,88},{56,96},{64,... | collective-permute-start | bytes 393224 | tf_op jit(solution)/shard_map/ppermute | solution.py:65
  742.6 19.6 %collective-permute-start.12 = (bf16[512,128]{1,0:T(8,128)(2,1)S(1)}, bf16[512,128]{1,0:T(8,128)(2,1)S(1)}, u32[]{:S(2)}, u32[]{:S(2)}) collective-permute-start(bf16[512,128]{1,0:T(8,128)(2,1)S(1)} %convolution_convert_fusion.1), channel_id=1, source_target_pairs={{0,32},{8,40},{16,48},{24,56},{32,64},{40,72},{48,80},{56,88},{64,... | collective-permute-start | bytes 393224 | tf_op jit(solution)/shard_map/ppermute | solution.py:65
  752.7 9.5 %collective-permute-start.13 = (bf16[512,128]{1,0:T(8,128)(2,1)S(1)}, bf16[512,128]{1,0:T(8,128)(2,1)S(1)}, u32[]{:S(2)}, u32[]{:S(2)}) collective-permute-start(bf16[512,128]{1,0:T(8,128)(2,1)S(1)} %convolution_convert_fusion.1), channel_id=1, source_target_pairs={{0,24},{8,32},{16,40},{24,48},{32,56},{40,64},{48,72},{56,80},{64,... | collective-permute-start | bytes 393224 | tf_op jit(solution)/shard_map/ppermute | solution.py:65
  757.1 6.9 collective-permute-start.14
  (26 other events, 933.1 us)
Sparse Core Ops, SparseCore 0:
  9.9 61.7 all-gather.16
  83.1 75.1 all-gather.18
  160.9 57.3 all-gather.20
  226.9 17.4 all-gather.24
  255.7 154.1 all-gather.26
  427.3 85.1 all-gather.28
  515.0 60.2 all-gather.14
  644.4 54.1 all-gather.22
where the time goes:
time: 818 us; the launch traced here: 817 us
  waiting for transfers between devices  540 us (66%)
  blocking collectives  92.3 us (11%)
  starting transfers between devices  54.7 us (7%)
  local copies, waits for them, and re-layouts  47.1 us (6%)
  matrix products  40.3 us (5%)
  other arithmetic  27 us (3%)
  between operations  15.1 us (2%)
    all_gather x3, waiting for transfers between devices, gathered_once(): both, at, found = (lax.all_gather(jnp.concatenate(lines), axis), 0, {})  238 us
    all_gather x1, waiting for transfers between devices, shards(): lax.all_gather(project(tokens, mem_key_w), 'head', axis=1, tiled=True)  61.9 us
    all_gather x1, waiting for transfers between devices, shards(): lax.all_gather(2.0 / tok_rows * (predicted - value_share), 'head', axis=0...  57.5 us
    all_to_all x1, blocking collectives, sent_and_summed(): lax.all_to_all(split_up(value, dim, length), axis, 0, 0, tiled=True)  56.2 us
    all_gather x1, waiting for transfers between devices, shards(): lax.all_gather(normalize(retrieved, norm_gain), 'head', axis=0, tiled=True)  54.3 us
    all_to_all x1, waiting for transfers between devices, sent_and_summed(): lax.all_to_all(split_up(value, dim, length), axis, 0, 0, tiled=True)  54.1 us
    ppermute x16, starting transfers between devices, shifted(): return lax.ppermute(value, axis, pairs)  50.5 us
    all_gather x1, waiting for transfers between devices, shards(): lax.all_gather(project(tokens, mem_query_w), 'head', axis=1, tiled=True)  48.5 us
  transfers between devices with their start and end apart: 25, of which 11 were waited for; matrix products, arithmetic and copies ran while one was open for 6% of the time, Pallas kernels for 0%

commit v1 on v0

--- a/solution.py
+++ b/solution.py
@@ -228,7 +228,11 @@
     weight_out = as_rows(entering[2]) * mem_out + entering[6]
     query_hidden = jax.nn.silu(jnp.dot(mem_query.astype(jnp.float32), weight_in))
     retrieved = sent_and_summed(jnp.dot(query_hidden, weight_out), "head", 0)
-    normed = lax.all_gather(normalize(retrieved, norm_gain), "head", axis=0, tiled=True)
+    part_2 = normalize(retrieved, norm_gain)
+    peers = lax.axis_size("head")
+    parts = jnp.stack([part_2 for _ in range(peers)])
+    parts = lax.all_to_all(parts, "head", split_axis=0, concat_axis=0)
+    normed = jnp.concatenate(parts, axis=0)
     att_query = project(normed, attn_query_w)
     att_key = project(normed, attn_key_w)
     att_value = project(normed, attn_value_w)

time: 818 us -> 788 us (0.963)
  waiting for transfers between devices: 540 us -> 508 us
    all_gather x1 -> x0, waiting for transfers between devices: 54.3 us -> none  [shards(): lax.all_gather(normalize(retrieved, norm_gain), 'head', axis=0, tiled=True)]
    all_to_all x0 -> x1, waiting for transfers between devices: none -> 23.7 us  [shards(): parts = lax.all_to_all(parts, 'head', split_axis=0, concat_axis=0)]
where the time goes in v1:
time: 788 us; the launch traced here: 786 us
  waiting for transfers between devices  508 us (64%)
  blocking collectives  90 us (11%)
  starting transfers between devices  60.3 us (8%)
  local copies, waits for them, and re-layouts  48.2 us (6%)
  matrix products  37.8 us (5%)
  other arithmetic  26.4 us (3%)
  between operations  15.1 us (2%)
    all_gather x3, waiting for transfers between devices, gathered_once(): both, at, found = (lax.all_gather(jnp.concatenate(lines), axis), 0, {})  238 us
    all_gather x1, waiting for transfers between devices, shards(): lax.all_gather(project(tokens, mem_key_w), 'head', axis=1, tiled=True)  61.9 us
    all_gather x1, waiting for transfers between devices, shards(): lax.all_gather(2.0 / tok_rows * (predicted - value_share), 'head', axis=0...  57.5 us
    all_to_all x1, blocking collectives, sent_and_summed(): lax.all_to_all(split_up(value, dim, length), axis, 0, 0, tiled=True)  56.4 us
    all_to_all x1, waiting for transfers between devices, sent_and_summed(): lax.all_to_all(split_up(value, dim, length), axis, 0, 0, tiled=True)  54.1 us
    ppermute x16, starting transfers between devices, shifted(): return lax.ppermute(value, axis, pairs)  52.4 us
    all_gather x1, waiting for transfers between devices, shards(): lax.all_gather(project(tokens, mem_query_w), 'head', axis=1, tiled=True)  48.6 us
    all_to_all x1, blocking collectives, sum_at_owner(): lax.all_to_all(split_up(value, dim, length), axis, 0, 0, tiled=True)  33.6 us
  transfers between devices with their start and end apart: 25, of which 11 were waited for; matrix products, arithmetic and copies ran while one was open for 6% of the time, Pallas kernels for 0%

profile of v1, /device:TPU:33, one launch (start us, length us, event | category | flops | bytes accessed | tf_op | source)
XLA Modules:
  0.0 786.0 jit_solution(1972052235393403069)
XLA Ops:
  9.8 61.9 %all-gather.16.cloned.1.call-done = bf16[512,1024]{1,0:T(8,128)(2,1)} async-done(((bf16[512,128]{1,0:T(8,128)(2,1)}), bf16[512,1024]{1,0:T(8,128)(2,1)}) %all-gather.16.cloned.1.call-update) | async-done | bytes 1048592 | tf_op jit(solution)/shard_map/all_gather | solution.py:196
  76.0 3.7 all-to-all-start
  81.0 54.1 %all-to-all-done = f32[8,64,1024]{2,1,0:T(8,128)S(1)} async-done(((f32[8,64,1024]{2,1,0:T(8,128)}), f32[8,64,1024]{2,1,0:T(8,128)S(1)}, u32[]{:S(2)}, u32[]{:S(2)}) %all-to-all-start) | async-done | bytes 2097184 | tf_op jit(solution)/shard_map/all_to_all | solution.py:20
  135.3 23.0 %all-gather.18.cloned.1.call-done = bf16[512,1024]{1,0:T(8,128)(2,1)} async-done(((bf16[512,128]{1,0:T(8,128)(2,1)}), bf16[512,1024]{1,0:T(8,128)(2,1)}) %all-gather.18.cloned.1.call-update) | async-done | bytes 1048592 | tf_op jit(solution)/shard_map/all_gather | solution.py:197
  160.7 57.5 %all-gather.20.cloned.1.call-done = bf16[512,1024]{1,0:T(8,128)(2,1)} async-done(((bf16[64,1024]{1,0:T(8,128)(2,1)}), bf16[512,1024]{1,0:T(8,128)(2,1)}) %all-gather.20.cloned.1.call-update) | async-done | bytes 1048592 | tf_op jit(solution)/shard_map/all_gather | solution.py:204
  222.7 4.1 concatenate.18
  226.9 17.6 %all-gather.22.cloned.1.call-done = f32[2,4099,128]{2,1,0:T(8,128)} async-done(((f32[1,4099,128]{2,1,0:T(8,128)}), f32[2,4099,128]{2,1,0:T(8,128)}) %all-gather.22.cloned.1.call-update) | async-done | bytes 4197392 | tf_op jit(solution)/shard_map/all_gather | solution.py:38
  251.5 4.1 concatenate.19
  255.7 154.2 %all-gather.24.cloned.1.call-done = f32[4,4099,128]{2,1,0:T(8,128)} async-done(((f32[1,4099,128]{2,1,0:T(8,128)}), f32[4,4099,128]{2,1,0:T(8,128)}) %all-gather.24.cloned.1.call-update) | async-done | bytes 8394768 | tf_op jit(solution)/shard_map/all_gather | solution.py:38
  419.0 4.0 bitcast_add_fusion
  423.1 4.1 concatenate.20
  446.6 65.9 %all-gather.26.cloned.1.call-done = f32[4,4099,128]{2,1,0:T(8,128)} async-done(((f32[1,4099,128]{2,1,0:T(8,128)}), f32[4,4099,128]{2,1,0:T(8,128)}) %all-gather.26.cloned.1.call-update) | async-done | bytes 8394768 | tf_op jit(solution)/shard_map/all_gather | solution.py:38
  526.8 48.6 %all-gather.14.cloned.1.call-done = bf16[512,1024]{1,0:T(8,128)(2,1)} async-done(((bf16[512,128]{1,0:T(8,128)(2,1)}), bf16[512,1024]{1,0:T(8,128)(2,1)}) %all-gather.14.cloned.1.call-update) | async-done | bytes 1048592 | tf_op jit(solution)/shard_map/all_gather | solution.py:195
  575.4 11.3 %fusion.57 = f32[512,1024]{1,0:T(8,128)} fusion(f32[128,1024]{1,0:T(8,128)} %squeeze.275, f32[128,1024]{1,0:T(8,128)} %squeeze.274, f32[128,1024]{1,0:T(8,128)} %squeeze.273, f32[128,1024]{1,0:T(8,128)} %squeeze.272, f32[128,1024]{1,0:T(8,128)} %squeeze.271, f32[128,1024]{1,0:T(8,128)} %squeeze.270, f32[128,1024]{1,0:T(8,128)} %squeeze.269, ...), kind=kOutput, calls=%fused_computation.101 | convolution fusion | flops 287834112 | bytes 25205248 | tf_op jit(solution)/shard_map/dot_general | solution.py:230
  586.7 56.4 %all_to_all.20 = f32[8,64,1024]{2,1,0:T(8,128)S(1)} all-to-all(f32[8,64,1024]{2,1,0:T(8,128)} %bitcast.565), channel_id=1, replica_groups=mesh['seq_0'=4,'seq_1'=4,'seq_2'=2,'head'=8] {'head'}, dimensions={0} | all-to-all | bytes 4194304 | tf_op jit(solution)/shard_map/all_to_all | solution.py:20
  645.0 3.7 all-to-all-start.2
  648.7 23.7 %all-to-all-done.2 = bf16[8,64,1024]{2,1,0:T(8,128)(2,1)S(1)} async-done(((bf16[8,64,1024]{2,1,0:T(8,128)(2,1)}), bf16[8,64,1024]{2,1,0:T(8,128)(2,1)S(1)}, u32[]{:S(2)}, u32[]{:S(2)}) %all-to-all-start.2) | async-done | bytes 1048608 | tf_op jit(solution)/shard_map/all_to_all | solution.py:234
  676.0 3.8 collective-permute-start.1
  681.1 6.3 collective-permute-start.3
  702.6 8.9 %collective-permute-start.10 = (bf16[512,128]{1,0:T(8,128)(2,1)S(1)}, bf16[512,128]{1,0:T(8,128)(2,1)S(1)}, u32[]{:S(2)}, u32[]{:S(2)}) collective-permute-start(bf16[512,128]{1,0:T(8,128)(2,1)S(1)} %convolution_convert_fusion.1), channel_id=1, source_target_pairs={{0,48},{8,56},{16,64},{24,72},{32,80},{40,88},{48,96},{56,104},{64... | collective-permute-start | bytes 393224 | tf_op jit(solution)/shard_map/ppermute | solution.py:65
  712.9 3.7 collective-permute-start.12
  716.7 4.3 fusion.356
  721.0 4.2 fusion.355
  744.8 33.6 %all_to_all.21 = bf16[8,512,128]{2,1,0:T(8,128)(2,1)S(1)} all-to-all(bf16[8,512,128]{2,1,0:T(8,128)(2,1)S(1)} %bitcast.564), channel_id=1, replica_groups=mesh['seq_0'=4,'seq_1'=4,'seq_2'=2,'head'=8] {'head'}, dimensions={0} | all-to-all | bytes 2097152 | tf_op jit(solution)/shard_map/all_to_all | solution.py:70
  (208 shorter events, 108.3 us)
Async XLA Ops:
  6.5 65.2 %all-gather.16.cloned.1.call-start = ((), (), s32[]{:S(2)}) async-start(), calls=%async_computation.5 | async-start | bytes 1179648 | tf_op jit(solution)/shard_map/all_gather | solution.py:196
  76.0 59.1 %all-to-all-start = ((f32[8,64,1024]{2,1,0:T(8,128)}), f32[8,64,1024]{2,1,0:T(8,128)S(1)}, u32[]{:S(2)}, u32[]{:S(2)}) async-start(f32[8,64,1024]{2,1,0:T(8,128)} %bitcast.563), calls=%async_computation | async-start | bytes 4194304 | tf_op jit(solution)/shard_map/all_to_all | solution.py:20
  79.8 78.5 %all-gather.18.cloned.1.call-start = ((), (), s32[]{:S(2)}) async-start(), calls=%async_computation.6 | async-start | bytes 1179648 | tf_op jit(solution)/shard_map/all_gather | solution.py:197
  81.0 137.3 %all-gather.20.cloned.1.call-start = ((), (), s32[]{:S(2)}) async-start(), calls=%async_computation.7 | async-start | bytes 1179648 | tf_op jit(solution)/shard_map/all_gather | solution.py:204
  159.9 84.5 %all-gather.22.cloned.1.call-start = ((), (), s32[]{:S(2)}) async-start(), calls=%async_computation.8 | async-start | bytes 6303744 | tf_op jit(solution)/shard_map/all_gather | solution.py:38
  226.8 183.1 %all-gather.24.cloned.1.call-start = ((), (), s32[]{:S(2)}) async-start(), calls=%async_computation.9 | async-start | bytes 10506240 | tf_op jit(solution)/shard_map/all_gather | solution.py:38
  255.6 256.9 %all-gather.26.cloned.1.call-start = ((), (), s32[]{:S(2)}) async-start(), calls=%async_computation.10 | async-start | bytes 10506240 | tf_op jit(solution)/shard_map/all_gather | solution.py:38
  427.2 148.2 %all-gather.14.cloned.1.call-start = ((), (), s32[]{:S(2)}) async-start(), calls=%async_computation.4 | async-start | bytes 1179648 | tf_op jit(solution)/shard_map/all_gather | solution.py:195
  645.0 27.4 %all-to-all-start.2 = ((bf16[8,64,1024]{2,1,0:T(8,128)(2,1)}), bf16[8,64,1024]{2,1,0:T(8,128)(2,1)S(1)}, u32[]{:S(2)}, u32[]{:S(2)}) async-start(bf16[8,64,1024]{2,1,0:T(8,128)(2,1)} %stack.2), calls=%async_computation.2 | async-start | bytes 2097152 | tf_op jit(solution)/shard_map/all_to_all | solution.py:234
  672.9 16.8 %collective-permute-start = (bf16[512,128]{1,0:T(8,128)(2,1)S(1)}, bf16[512,128]{1,0:T(8,128)(2,1)S(1)}, u32[]{:S(2)}, u32[]{:S(2)}) collective-permute-start(bf16[512,128]{1,0:T(8,128)(2,1)S(1)} %convolution_convert_fusion.2), channel_id=1, source_target_pairs={{0,64},{8,72},{16,80},{24,88},{32,96},{40,104},{48,112},{56,120},{... | collective-permute-start | bytes 393224 | tf_op jit(solution)/shard_map/ppermute | solution.py:65
  676.0 17.4 %collective-permute-start.1 = (bf16[512,128]{1,0:T(8,128)(2,1)S(1)}, bf16[512,128]{1,0:T(8,128)(2,1)S(1)}, u32[]{:S(2)}, u32[]{:S(2)}) collective-permute-start(bf16[512,128]{1,0:T(8,128)(2,1)S(1)} %convolution_convert_fusion.2), channel_id=1, source_target_pairs={{0,56},{8,64},{16,72},{24,80},{32,88},{40,96},{48,104},{56,112},{6... | collective-permute-start | bytes 393224 | tf_op jit(solution)/shard_map/ppermute | solution.py:65
  679.8 15.9 %collective-permute-start.2 = (bf16[512,128]{1,0:T(8,128)(2,1)S(1)}, bf16[512,128]{1,0:T(8,128)(2,1)S(1)}, u32[]{:S(2)}, u32[]{:S(2)}) collective-permute-start(bf16[512,128]{1,0:T(8,128)(2,1)S(1)} %convolution_convert_fusion.2), channel_id=1, source_target_pairs={{0,48},{8,56},{16,64},{24,72},{32,80},{40,88},{48,96},{56,104},{64... | collective-permute-start | bytes 393224 | tf_op jit(solution)/shard_map/ppermute | solution.py:65
  681.1 18.3 %collective-permute-start.3 = (bf16[512,128]{1,0:T(8,128)(2,1)S(1)}, bf16[512,128]{1,0:T(8,128)(2,1)S(1)}, u32[]{:S(2)}, u32[]{:S(2)}) collective-permute-start(bf16[512,128]{1,0:T(8,128)(2,1)S(1)} %convolution_convert_fusion.2), channel_id=1, source_target_pairs={{0,40},{8,48},{16,56},{24,64},{32,72},{40,80},{48,88},{56,96},{64,... | collective-permute-start | bytes 393224 | tf_op jit(solution)/shard_map/ppermute | solution.py:65
  687.3 13.4 %collective-permute-start.4 = (bf16[512,128]{1,0:T(8,128)(2,1)S(1)}, bf16[512,128]{1,0:T(8,128)(2,1)S(1)}, u32[]{:S(2)}, u32[]{:S(2)}) collective-permute-start(bf16[512,128]{1,0:T(8,128)(2,1)S(1)} %convolution_convert_fusion.2), channel_id=1, source_target_pairs={{0,32},{8,40},{16,48},{24,56},{32,64},{40,72},{48,80},{56,88},{64,... | collective-permute-start | bytes 393224 | tf_op jit(solution)/shard_map/ppermute | solution.py:65
  689.7 12.9 %collective-permute-start.5 = (bf16[512,128]{1,0:T(8,128)(2,1)S(1)}, bf16[512,128]{1,0:T(8,128)(2,1)S(1)}, u32[]{:S(2)}, u32[]{:S(2)}) collective-permute-start(bf16[512,128]{1,0:T(8,128)(2,1)S(1)} %convolution_convert_fusion.2), channel_id=1, source_target_pairs={{0,24},{8,32},{16,40},{24,48},{32,56},{40,64},{48,72},{56,80},{64,... | collective-permute-start | bytes 393224 | tf_op jit(solution)/shard_map/ppermute | solution.py:65
  693.4 18.2 %collective-permute-start.6 = (bf16[512,128]{1,0:T(8,128)(2,1)S(1)}, bf16[512,128]{1,0:T(8,128)(2,1)S(1)}, u32[]{:S(2)}, u32[]{:S(2)}) collective-permute-start(bf16[512,128]{1,0:T(8,128)(2,1)S(1)} %convolution_convert_fusion.2), channel_id=1, source_target_pairs={{0,16},{8,24},{16,32},{24,40},{32,48},{40,56},{48,64},{56,72},{64,... | collective-permute-start | bytes 393224 | tf_op jit(solution)/shard_map/ppermute | solution.py:65
  695.7 17.2 %collective-permute-start.7 = (bf16[512,128]{1,0:T(8,128)(2,1)S(1)}, bf16[512,128]{1,0:T(8,128)(2,1)S(1)}, u32[]{:S(2)}, u32[]{:S(2)}) collective-permute-start(bf16[512,128]{1,0:T(8,128)(2,1)S(1)} %convolution_convert_fusion.2), channel_id=1, source_target_pairs={{0,8},{8,16},{16,24},{24,32},{32,40},{40,48},{48,56},{56,64},{64,7... | collective-permute-start | bytes 393224 | tf_op jit(solution)/shard_map/ppermute | solution.py:65
  699.4 25.8 %collective-permute-start.8 = (bf16[512,128]{1,0:T(8,128)(2,1)S(1)}, bf16[512,128]{1,0:T(8,128)(2,1)S(1)}, u32[]{:S(2)}, u32[]{:S(2)}) collective-permute-start(bf16[512,128]{1,0:T(8,128)(2,1)S(1)} %convolution_convert_fusion.1), channel_id=1, source_target_pairs={{0,64},{8,72},{16,80},{24,88},{32,96},{40,104},{48,112},{56,120},{... | collective-permute-start | bytes 393224 | tf_op jit(solution)/shard_map/ppermute | solution.py:65
  700.7 28.1 %collective-permute-start.9 = (bf16[512,128]{1,0:T(8,128)(2,1)S(1)}, bf16[512,128]{1,0:T(8,128)(2,1)S(1)}, u32[]{:S(2)}, u32[]{:S(2)}) collective-permute-start(bf16[512,128]{1,0:T(8,128)(2,1)S(1)} %convolution_convert_fusion.1), channel_id=1, source_target_pairs={{0,56},{8,64},{16,72},{24,80},{32,88},{40,96},{48,104},{56,112},{6... | collective-permute-start | bytes 393224 | tf_op jit(solution)/shard_map/ppermute | solution.py:65
  702.6 29.0 %collective-permute-start.10 = (bf16[512,128]{1,0:T(8,128)(2,1)S(1)}, bf16[512,128]{1,0:T(8,128)(2,1)S(1)}, u32[]{:S(2)}, u32[]{:S(2)}) collective-permute-start(bf16[512,128]{1,0:T(8,128)(2,1)S(1)} %convolution_convert_fusion.1), channel_id=1, source_target_pairs={{0,48},{8,56},{16,64},{24,72},{32,80},{40,88},{48,96},{56,104},{64... | collective-permute-start | bytes 393224 | tf_op jit(solution)/shard_map/ppermute | solution.py:65
  711.6 23.8 %collective-permute-start.11 = (bf16[512,128]{1,0:T(8,128)(2,1)S(1)}, bf16[512,128]{1,0:T(8,128)(2,1)S(1)}, u32[]{:S(2)}, u32[]{:S(2)}) collective-permute-start(bf16[512,128]{1,0:T(8,128)(2,1)S(1)} %convolution_convert_fusion.1), channel_id=1, source_target_pairs={{0,40},{8,48},{16,56},{24,64},{32,72},{40,80},{48,88},{56,96},{64,... | collective-permute-start | bytes 393224 | tf_op jit(solution)/shard_map/ppermute | solution.py:65
  712.9 22.5 %collective-permute-start.12 = (bf16[512,128]{1,0:T(8,128)(2,1)S(1)}, bf16[512,128]{1,0:T(8,128)(2,1)S(1)}, u32[]{:S(2)}, u32[]{:S(2)}) collective-permute-start(bf16[512,128]{1,0:T(8,128)(2,1)S(1)} %convolution_convert_fusion.1), channel_id=1, source_target_pairs={{0,32},{8,40},{16,48},{24,56},{32,64},{40,72},{48,80},{56,88},{64,... | collective-permute-start | bytes 393224 | tf_op jit(solution)/shard_map/ppermute | solution.py:65
  725.2 10.2 %collective-permute-start.13 = (bf16[512,128]{1,0:T(8,128)(2,1)S(1)}, bf16[512,128]{1,0:T(8,128)(2,1)S(1)}, u32[]{:S(2)}, u32[]{:S(2)}) collective-permute-start(bf16[512,128]{1,0:T(8,128)(2,1)S(1)} %convolution_convert_fusion.1), channel_id=1, source_target_pairs={{0,24},{8,32},{16,40},{24,48},{32,56},{40,64},{48,72},{56,80},{64,... | collective-permute-start | bytes 393224 | tf_op jit(solution)/shard_map/ppermute | solution.py:65
  728.8 6.9 collective-permute-start.14
  (25 other events, 820.1 us)
Sparse Core Ops, SparseCore 0:
  9.9 61.7 all-gather.15
  83.1 75.1 all-gather.17
  160.9 57.3 all-gather.19
  226.9 17.4 all-gather.21
  255.7 154.1 all-gather.23
  427.3 85.1 all-gather.25
  515.0 60.2 all-gather.13
